TPU v7x, 128 devices: a whole 4x4x4 slice. The times are simulated.
128 devices in a mesh: nodes: 2 (over core), gx: 8 (over y_lo, z), gy: 8 (over y_hi, x).
Axes of the slice: x: 4, y: 4 (y_hi: 2, y_lo: 2; y = y_hi * 2 + y_lo), z: 4, core: 2. Of those that a mesh axis runs over, the one named last changes fastest.
Arguments:
- field_modes: float32 [4, 9, 512, 1024], P(None, None, 'gx', 'gy'), may hold values from -4 to 4, as said below
- node_points: float32 [768, 8], replicated, may hold values from -1 to 1
- quad_weight: float32 [768], replicated, may hold values from 0.5 to 2
- group_of: int32 [768], replicated, may hold values from 0 to 2, as said below
Outputs:
- mean_field: float32 [512, 1024], P('gx', 'gy')
- variance_field: float32 [512, 1024], P('gx', 'gy')
Inputs may be any that keep to these rules, and one draw needn't show every extreme that they name: `group_of`: one of the two groups (which one varies) is given exactly 384 nodes, the other between 48 and 96; all other nodes hold 2. `field_modes`: diffusivity fields (index 3) give a diffusivity between 0.1 and 1.4 at every node point in range; the other fields lie within the range.
All inputs are finite; a program needn't handle non-finite values.
Results may differ from a plain program's by a relative error of at most 0.00021.
Values sent between devices are 32-bit elements; how exact they have to be, the bound alone decides.
A program may use at most 192 MiB of HBM per device.

v0:
```python
import functools

import jax
import jax.numpy as jnp
from jax import lax
from jax.experimental import pallas as pl
from jax.experimental.pallas import tpu as pltpu
from jax.sharding import PartitionSpec as P

TIME_STEP = 0.15
HALO = 4
LANES = 128
SUBLANES = 8
SLOTS = 256
MESH = pl.DeviceIdType.MESH
F32 = jnp.float32
BF16 = jnp.bfloat16


def nn(a, b):
    return lax.dot_general(a, b, (((1,), (0,)), ((), ())), preferred_element_type=F32)


def nt(a, b):
    return lax.dot_general(a, b, (((1,), (1,)), ((), ())), preferred_element_type=F32)


def split2(x):
    hi = x.astype(BF16).astype(F32)
    return hi, x - hi


def split3(x):
    hi = x.astype(BF16).astype(F32)
    rest = x - hi
    mid = rest.astype(BF16).astype(F32)
    return hi, mid, rest - mid


def kernel(
    gx_size, gy_size, rows, dims,
    field_hbm, points_ref, weight_ref, group_ref,
    total_ref, wsum_ref,
    fv, send_rows, recv_rows, send_cols, recv_cols, lhs, cols_t, rhs, node_w,
    cf0, cf1, u0a, u0b, u1, u2, u3, part, acc, nat, mine, theirs, csc,
    load_sem, send_sem, recv_sem,
):
    ext = rows + 2 * HALO
    pairs = ext // 2
    modes = dims + 1
    fields = 4 * modes
    ring = LANES + 2 * HALO
    chunk = ring // SUBLANES
    kpad = 40
    core = lax.axis_index("nodes")
    gx = lax.axis_index("gx")
    gy = lax.axis_index("gy")
    xn, xp = lax.rem(gx + 1, gx_size), lax.rem(gx + gx_size - 1, gx_size)
    yn, yp = lax.rem(gy + 1, gy_size), lax.rem(gy + gy_size - 1, gy_size)
    around = [
        (core, xp, gy), (core, xn, gy), (core, gx, yp), (core, gx, yn),
        (core, xp, yp), (core, xp, yn), (core, xn, yp), (core, xn, yn),
        (1 - core, gx, gy),
    ]

    load = pltpu.make_async_copy(field_hbm, fv.at[pl.ds(0, fields * rows)], load_sem)
    load.start()
    barrier = pltpu.get_barrier_semaphore()
    for device in around:
        pl.semaphore_signal(barrier, inc=1, device_id=device, device_id_type=MESH)

    fv[pl.ds(fields * rows, (kpad - fields) * rows), :] = jnp.zeros(((kpad - fields) * rows, LANES), F32)
    load.wait()

    for r in range(HALO):
        send_rows[0, pl.ds(r, kpad, stride=HALO), :] = fv[pl.ds(r, kpad, stride=rows), :]
        send_rows[1, pl.ds(r, kpad, stride=HALO), :] = fv[pl.ds(rows - HALO + r, kpad, stride=rows), :]
    lane = lax.broadcasted_iota(jnp.int32, (kpad, LANES), 1)
    per_tile = LANES // HALO
    tiles = rows // per_tile
    for t in range(tiles):
        low = jnp.zeros((kpad, LANES), F32)
        high = jnp.zeros((kpad, LANES), F32)
        for g in range(per_tile):
            x = fv[pl.ds(t * per_tile + g, kpad, stride=rows), :]
            x = pltpu.roll(x, (HALO * (g + 1)) % LANES, 1)
            high = jnp.where(lane // HALO == g, x, high)
            low = jnp.where(lane // HALO == (g + 1) % per_tile, x, low)
        send_cols[0, t] = low
        send_cols[1, t] = high

    pl.semaphore_wait(barrier, len(around))

    def remote(index, source, target, device):
        copy = pltpu.make_async_remote_copy(
            src_ref=source, dst_ref=target,
            send_sem=send_sem.at[index], recv_sem=recv_sem.at[index],
            device_id=device, device_id_type=MESH,
        )
        copy.start()
        return copy

    last = tiles - 1
    copies = [
        remote(2, send_cols.at[0], recv_cols.at[pl.ds(0, tiles)], (core, gx, yp)),
        remote(3, send_cols.at[1], recv_cols.at[pl.ds(tiles, tiles)], (core, gx, yn)),
        remote(0, send_rows.at[0], recv_rows.at[0], (core, xp, gy)),
        remote(1, send_rows.at[1], recv_rows.at[1], (core, xn, gy)),
        remote(4, send_cols.at[0, 0], recv_cols.at[2 * tiles], (core, xp, yp)),
        remote(5, send_cols.at[1, 0], recv_cols.at[2 * tiles + 1], (core, xp, yn)),
        remote(6, send_cols.at[0, last], recv_cols.at[2 * tiles + 2], (core, xn, yp)),
        remote(7, send_cols.at[1, last], recv_cols.at[2 * tiles + 3], (core, xn, yn)),
    ]

    count = group_ref.shape[1]
    included = (group_ref[...] < 2).astype(F32)
    weights = weight_ref[...]
    wsum_ref[...] = jnp.broadcast_to(jnp.sum(weights * included, axis=1, keepdims=True), wsum_ref.shape)
    before = lax.broadcasted_iota(jnp.int32, (count, count), 0) <= lax.broadcasted_iota(jnp.int32, (count, count), 1)
    order = nn(jnp.broadcast_to(included, (SUBLANES, count)).astype(BF16), before.astype(F32).astype(BF16))[0:1]
    slot = (lax.broadcasted_iota(jnp.int32, (SLOTS, count), 0) + (core * SLOTS + 1)).astype(F32)
    chosen = jnp.where(slot == jnp.broadcast_to(order, (SLOTS, count)), jnp.broadcast_to(included, (SLOTS, count)), 0.0)
    select = chosen.astype(BF16)
    eye = (
        lax.broadcasted_iota(jnp.int32, (SUBLANES, dims), 0) == lax.broadcasted_iota(jnp.int32, (SUBLANES, dims), 1)
    ).astype(F32).astype(BF16)
    coords = jnp.zeros((SUBLANES, SLOTS), F32)
    for piece in split3(points_ref[...]):
        picked = nn(select, piece.astype(BF16))
        coords = coords + nt(eye, picked.astype(BF16))
    held = jnp.zeros((SUBLANES, SLOTS), F32)
    for piece in split3(weights):
        held = held + nt(jnp.broadcast_to(piece, (SUBLANES, count)).astype(BF16), select)
    node_w[...] = held

    csc[...] = jnp.zeros_like(csc)
    csc[0:1, :] = jnp.ones((1, SLOTS), F32)
    csc[1 : 1 + dims, :] = coords
    coefficient = csc[...][0:modes]
    rhs[...] = jnp.zeros_like(rhs)

    def place(output, field, scale):
        hi, lo = split2(coefficient * scale)
        for h in range(2):
            lanes = pl.ds((output % 2) * LANES, LANES)
            at = field * modes
            part_hi = hi[:, h * LANES : (h + 1) * LANES]
            part_lo = lo[:, h * LANES : (h + 1) * LANES]
            rhs[h, output // 2, pl.ds(at, modes), lanes] = part_hi
            rhs[h, output // 2, pl.ds(kpad + at, modes), lanes] = part_lo
            rhs[h, output // 2, pl.ds(2 * kpad + at, modes), lanes] = part_hi

    diffuse, move = TIME_STEP, 0.5 * TIME_STEP
    for output, (field, sign) in enumerate([(None, 0), (1, -1), (1, 1), (2, -1), (2, 1)]):
        place(output, 3, -4.0 * diffuse if field is None else diffuse)
        if field is not None:
            place(output, field, sign * move)
    place(5, 0, 1.0)
    rhs[0, 0, 3 * kpad : 3 * kpad + 1, 0:LANES] = jnp.ones((1, LANES), F32)
    rhs[1, 0, 3 * kpad : 3 * kpad + 1, 0:LANES] = jnp.ones((1, LANES), F32)

    ones = jnp.where(lax.broadcasted_iota(jnp.int32, (SUBLANES, LANES), 0) == 0, 1.0, 0.0)

    def turned(x):
        hi, lo = split2(x)
        return jnp.transpose(jnp.concatenate([hi, hi, lo, ones], axis=0))

    @pl.loop(0, rows // 2)
    def _(pair):
        for half in range(2):
            row = 2 * pair + half
            at = pl.multiple_of((row + HALO) * ring, SUBLANES)
            lhs[pl.ds(at, LANES), :] = turned(fv[pl.ds(row, kpad, stride=rows), :])

    acc[...] = jnp.zeros_like(acc)

    for copy in copies:
        copy.wait_recv()

    for r in range(HALO):
        up = turned(recv_rows[1, pl.ds(r, kpad, stride=HALO), :])
        lhs[pl.ds(r * ring, LANES), :] = up
        down = turned(recv_rows[0, pl.ds(r, kpad, stride=HALO), :])
        lhs[pl.ds((rows + HALO + r) * ring, LANES), :] = down
    for t in range(2 * tiles + 4):
        cols_t[pl.ds(t * LANES, LANES), :] = turned(recv_cols[t])

    def column_halo(row, right, left):
        base = row * ring + LANES
        lhs[pl.ds(base, HALO), :] = cols_t[pl.ds(right, HALO), :]
        lhs[pl.ds(base + HALO, HALO), :] = cols_t[pl.ds(left, HALO), :]

    for row in range(rows):
        t, g = divmod(row, per_tile)
        column_halo(
            row + HALO,
            t * LANES + HALO * ((g + 1) % per_tile),
            (tiles + t) * LANES + HALO * g,
        )
    for r in range(HALO):
        corner = 2 * tiles * LANES
        column_halo(rows + HALO + r, corner + HALO * (r + 1), corner + LANES + HALO * r)
        g = per_tile - HALO + r
        column_halo(r, corner + 2 * LANES + HALO * ((g + 1) % per_tile), corner + 3 * LANES + HALO * g)

    cfs = (cf0, cf1)
    u0s = (u0a, u0b)
    states = (u0s, (u1.at[0], u1.at[1]), (u2.at[0], u2.at[1]), (u3.at[0], u3.at[1]))
    cf_ring, u_ring = cf0.shape[1], u0a.shape[0]

    def parameters(h, pair):
        pieces = []
        for half in range(2):
            base = (2 * pair + half) * ring
            pieces += [lhs[pl.ds(base + j, SUBLANES, stride=chunk), :] for j in range(chunk)]
        left = jnp.concatenate(pieces, axis=0)
        cslot = lax.rem(2 * pair, cf_ring)
        uslot = lax.rem(2 * pair, u_ring)
        for g in range(3):
            found = nn(left, rhs[h, g])
            for half in range(2):
                cut = found[half * ring : (half + 1) * ring]
                cfs[h][2 * g, cslot + half] = cut[:, 0:LANES]
                if g < 2:
                    cfs[h][2 * g + 1, cslot + half] = cut[:, LANES:]
                else:
                    u0s[h][uslot + half] = cut[:, LANES:]

    lane_of = lax.broadcasted_iota(jnp.int32, (SUBLANES, LANES), 1)
    tile = [pl.ds(SUBLANES * j, SUBLANES) for j in range(chunk)]

    def advance(step, h, pair):
        source = states[step - 1][h]
        slots = [lax.rem(2 * pair + u_ring - 1 + k, u_ring) for k in range(4)]
        cslot = lax.rem(2 * pair, cf_ring)
        below = [source[slots[0], tile[j], :] for j in range(chunk)]
        here = [source[slots[1], tile[j], :] for j in range(chunk)]
        for half in range(2):
            above = [source[slots[half + 2], tile[j], :] for j in range(chunk)]
            for j in range(chunk):
                north = here[j + 1] if j + 1 < chunk else pltpu.roll(here[0], SUBLANES - 1, 0)
                south = here[j - 1] if j else pltpu.roll(here[chunk - 1], 1, 0)
                c = [cfs[h][k, cslot + half, tile[j], :] for k in range(5)]
                new = (c[0] * here[j] + c[1] * above[j]) + c[2] * below[j] + (c[3] * north + c[4] * south)
                if step < 4:
                    states[step][h][slots[1 + half], tile[j], :] = new
                    continue
                w = node_w[:, h * LANES : (h + 1) * LANES]
                one = w * new
                two = one * new
                if h == 0:
                    part[half, 0, tile[j], :] = one
                    part[half, 1, tile[j], :] = two
                else:
                    row = 2 * pair + half - HALO
                    one = jnp.sum(one + part[half, 0, tile[j], :], axis=1, keepdims=True)
                    two = jnp.sum(two + part[half, 1, tile[j], :], axis=1, keepdims=True)
                    old = acc[tile[j], :]
                    old = jnp.where(lane_of == row, one, old)
                    acc[tile[j], :] = jnp.where(lane_of == row + rows, two, old)
            below, here = here, above

    lag = 2
    for pair in range(2):
        for h in range(2):
            parameters(h, pair)

    spans = {
        0: (0, pairs - 2),
        1: (0, pairs),
        2: (1 + lag, pairs - 1 + lag),
        3: (1 + 2 * lag, pairs - 1 + 2 * lag),
        4: (2 + 3 * lag, pairs - 2 + 3 * lag),
    }
    cuts = sorted({x for span in spans.values() for x in span})
    for first, final in zip(cuts[:-1], cuts[1:]):
        active = [k for k, (a, b) in spans.items() if a <= first and final <= b]

        @pl.loop(first, final)
        def _(q):
            for h in range(2):
                for step in (4, 3, 2, 1):
                    if step in active:
                        advance(step, h, q - lag * (step - 1))
                if 0 in active:
                    parameters(1 - h, q + 2)

    for j in range(chunk):
        nat[pl.ds(j, SUBLANES, stride=chunk), :] = acc[tile[j], :]
    mine[...] = jnp.transpose(nat[0:LANES, :])
    swap = remote(8, mine, theirs, (1 - core, gx, gy))
    for copy in copies:
        copy.wait_send()
    swap.wait()
    total_ref[...] = mine[...] + theirs[...]


def on_device(mesh, field_modes, node_points, quad_weight, group_of):
    rows, cols = field_modes.shape[2:]
    count, dims = node_points.shape
    modes = dims + 1
    ext = rows + 2 * HALO
    ring = cols + 2 * HALO
    kpad = 40
    tiles = rows * HALO // LANES
    vmem = pl.BlockSpec(memory_space=pltpu.VMEM)
    total, wsum = pl.pallas_call(
        functools.partial(kernel, mesh.shape["gx"], mesh.shape["gy"], rows, dims),
        out_shape=(
            jax.ShapeDtypeStruct((2 * rows, cols), F32),
            jax.ShapeDtypeStruct((SUBLANES, LANES), F32),
        ),
        in_specs=[pl.BlockSpec(memory_space=pl.ANY), vmem, vmem, vmem],
        out_specs=(vmem, vmem),
        scratch_shapes=[
            pltpu.VMEM((kpad * rows, LANES), F32),
            pltpu.VMEM((2, kpad * HALO, LANES), F32),
            pltpu.VMEM((2, kpad * HALO, LANES), F32),
            pltpu.VMEM((2, tiles, kpad, LANES), F32),
            pltpu.VMEM((2 * tiles + 4, kpad, LANES), F32),
            pltpu.VMEM((ext * ring, LANES), F32),
            pltpu.VMEM(((2 * tiles + 4) * LANES, LANES), F32),
            pltpu.VMEM((2, 3, LANES, 2 * LANES), F32),
            pltpu.VMEM((SUBLANES, SLOTS), F32),
            pltpu.VMEM((5, 32, ring, LANES), F32),
            pltpu.VMEM((5, 32, ring, LANES), F32),
            pltpu.VMEM((8, ring, LANES), F32),
            pltpu.VMEM((8, ring, LANES), F32),
            pltpu.VMEM((2, 8, ring, LANES), F32),
            pltpu.VMEM((2, 8, ring, LANES), F32),
            pltpu.VMEM((2, 8, ring, LANES), F32),
            pltpu.VMEM((2, 2, ring, LANES), F32),
            pltpu.VMEM((ring, LANES), F32),
            pltpu.VMEM((ring, LANES), F32),
            pltpu.VMEM((2 * rows, LANES), F32),
            pltpu.VMEM((2 * rows, LANES), F32),
            pltpu.VMEM((2 * SUBLANES, SLOTS), F32),
            pltpu.SemaphoreType.DMA,
            pltpu.SemaphoreType.DMA((9,)),
            pltpu.SemaphoreType.DMA((9,)),
        ],
        compiler_params=pltpu.CompilerParams(
            collective_id=0, has_side_effects=True, vmem_limit_bytes=60 * 1024 * 1024
        ),
    )(
        field_modes.reshape(4 * modes * rows, cols),
        node_points,
        quad_weight.reshape(1, count),
        group_of.reshape(1, count),
    )
    weight_total = wsum[0, 0]
    mean_field = total[:rows] / weight_total
    variance_field = total[rows:] / weight_total - mean_field * mean_field
    return mean_field, variance_field


def solution(mesh):
    return jax.shard_map(
        functools.partial(on_device, mesh),
        mesh=mesh,
        in_specs=(P(None, None, "gx", "gy"), P(), P(), P()),
        out_specs=(P("gx", "gy"), P("gx", "gy")),
        check_vma=False,
    )
```

profile of v0, /device:TPU:1, one launch (start us, length us, event | category | flops | bytes accessed | tf_op | source)
XLA Modules:
  0.0 62.6 jit_solution(15782356356973561475)
XLA Ops:
  0.6 1.3 %reshape.14.weight_ref = f32[1,768]{1,0:T(1,128)} reshape(f32[768]{0:T(1024)} %param.6) | data formatting | bytes 6144 | tf_op jit(solution)/shard_map/reshape | solution.py:348
  1.9 1.3 %reshape.15.group_ref = s32[1,768]{1,0:T(1,128)} reshape(s32[768]{0:T(1024)} %param.7) | data formatting | bytes 6144 | tf_op jit(solution)/shard_map/reshape | solution.py:349
  3.2 1.6 %copy.6.points_ref = f32[768,8]{1,0:T(8,128)} copy(f32[768,8]{0,1:T(8,128)} %param.5) | data formatting | bytes 49152 | tf_op args[1]
  4.8 54.5 %shard_map.59 = (f32[128,128]{1,0:T(8,128)}, f32[8,128]{1,0:T(8,128)}) custom-call(f32[2304,128]{1,0:T(8,128)} %bitcast.2, f32[768,8]{1,0:T(8,128)} %copy.6.points_ref, f32[1,768]{1,0:T(1,128)} %reshape.14.weight_ref, s32[1,768]{1,0:T(1,128)} %reshape.15.group_ref), custom_call_target="tpu_custom_call" | custom-call | tf_op jit(solution)/shard_map/pallas_call | solution.py:307
  59.3 1.2 %slice.10 = f32[1,1]{1,0:T(1,128)} slice(f32[8,128]{1,0:T(8,128)} %get-tuple-element.5), slice={[0:1], [0:1]} | slice | bytes 8 | tf_op jit(solution)/shard_map/slice | solution.py:351
  60.5 2.0 %multiply_subtract_fusion = (f32[64,128]{1,0:T(8,128)}, f32[64,128]{1,0:T(8,128)}) fusion(f32[128,128]{1,0:T(8,128)} %get-tuple-element.4, f32[]{:T(128)} %bitcast.1), kind=kLoop, calls=%fused_computation | loop fusion | flops 32768 | bytes 131076 | tf_op jit(solution)/shard_map/sub | solution.py:353
where the time goes:
time: 63 us; the launch traced here: 62.6 us
  Pallas kernels  54.5 us (87%)
  local copies, waits for them, and re-layouts  5.4 us (9%)
  other arithmetic  2.04 us (3%)
  between operations  0.64 us (1%)
    pallas_call x1, Pallas kernels, on_device(): pl.pallas_call(functools.partial(kernel, mesh.shape['gx'], mesh.shape['gy...  54.5 us
    sub x1, other arithmetic, on_device(): variance_field = total[rows:] / weight_total - mean_field * mean_field  2.04 us
    unnamed x1, local copies, waits for them, and re-layouts  1.65 us
    reshape x1, local copies, waits for them, and re-layouts, on_device(): quad_weight.reshape(1, count)  1.27 us
    reshape x1, local copies, waits for them, and re-layouts, on_device(): group_of.reshape(1, count)  1.27 us

commit v1 on v0

v1 whole, which is shorter than its diff:
```python
import functools

import jax
import jax.numpy as jnp
from jax import lax
from jax.experimental import pallas as pl
from jax.experimental.pallas import tpu as pltpu
from jax.sharding import PartitionSpec as P

TIME_STEP = 0.15
HALO = 4
LANES = 128
SUBLANES = 8
SLOTS = 256
ROWS = 4
MESH = pl.DeviceIdType.MESH
F32 = jnp.float32
BF16 = jnp.bfloat16


def nn(a, b):
    return lax.dot_general(a, b, (((1,), (0,)), ((), ())), preferred_element_type=F32)


def nt(a, b):
    return lax.dot_general(a, b, (((1,), (1,)), ((), ())), preferred_element_type=F32)


def split2(x):
    hi = x.astype(BF16).astype(F32)
    return hi, x - hi


def split3(x):
    hi = x.astype(BF16).astype(F32)
    rest = x - hi
    mid = rest.astype(BF16).astype(F32)
    return hi, mid, rest - mid


def kernel(
    gx_size, gy_size, rows, dims,
    field_hbm, points_ref, weight_ref, group_ref,
    moments_ref,
    fv, send_rows, recv_rows, send_cols, recv_cols, send_corners, recv_corners,
    lnat, left, cols_t, halo_l, rhs_f, rhs, node_w, csc,
    cf0, cf1, ua, ub, kept, part, both, acc, nat, mine, theirs,
    load_sem, send_sem, recv_sem,
):
    ext = rows + 2 * HALO
    quads = ext // ROWS
    modes = dims + 1
    fields = 4 * modes
    ring = LANES + 2 * HALO
    chunk = ring // SUBLANES
    kpad = 40
    groups = kpad // SUBLANES
    core = lax.axis_index("nodes")
    gx = lax.axis_index("gx")
    gy = lax.axis_index("gy")
    xn, xp = lax.rem(gx + 1, gx_size), lax.rem(gx + gx_size - 1, gx_size)
    yn, yp = lax.rem(gy + 1, gy_size), lax.rem(gy + gy_size - 1, gy_size)
    around = [
        (core, xp, gy), (core, xn, gy), (core, gx, yp), (core, gx, yn),
        (core, xp, yp), (core, xp, yn), (core, xn, yp), (core, xn, yn),
        (1 - core, gx, gy),
    ]

    load = pltpu.make_async_copy(field_hbm, fv.at[pl.ds(0, fields * rows)], load_sem)
    load.start()
    barrier = pltpu.get_barrier_semaphore()
    for device in around:
        pl.semaphore_signal(barrier, inc=1, device_id=device, device_id_type=MESH)

    fv[pl.ds(fields * rows, (kpad - fields) * rows), :] = jnp.zeros(((kpad - fields) * rows, LANES), F32)
    load.wait()

    for r in range(HALO):
        send_rows[0, pl.ds(r, kpad, stride=HALO), :] = fv[pl.ds(r, kpad, stride=rows), :]
        send_rows[1, pl.ds(r, kpad, stride=HALO), :] = fv[pl.ds(rows - HALO + r, kpad, stride=rows), :]
    lane = lax.broadcasted_iota(jnp.int32, (SUBLANES, LANES), 1)
    by_halo = lane // HALO
    block = HALO * HALO
    by_block = lane // block
    per_tile = LANES // HALO
    tiles = rows // per_tile
    for t in range(tiles):
        low = [jnp.zeros((SUBLANES, LANES), F32)] * groups
        high = [jnp.zeros((SUBLANES, LANES), F32)] * groups
        for g in range(per_tile):
            at_high = by_halo == g
            at_low = by_halo == (g + 1) % per_tile
            for m in range(groups):
                x = fv[pl.ds(m * SUBLANES * rows + t * per_tile + g, SUBLANES, stride=rows), :]
                x = pltpu.roll(x, (HALO * (g + 1)) % LANES, 1)
                high[m] = jnp.where(at_high, x, high[m])
                low[m] = jnp.where(at_low, x, low[m])
        for side, values in enumerate((low, high)):
            for m in range(groups):
                send_cols[side, t, m * SUBLANES : (m + 1) * SUBLANES, :] = values[m]
            for end in range(2):
                if t != (0, tiles - 1)[end]:
                    continue
                at = HALO * (1 - side) + (0, LANES - block)[end]
                packed = jnp.zeros((SUBLANES, LANES), F32)
                for m in range(groups):
                    packed = jnp.where(by_block == m, pltpu.roll(values[m], (block * m - at) % LANES, 1), packed)
                send_corners[2 * end + side] = packed

    pl.semaphore_wait(barrier, len(around))

    def remote(index, source, target, device):
        copy = pltpu.make_async_remote_copy(
            src_ref=source, dst_ref=target,
            send_sem=send_sem.at[index], recv_sem=recv_sem.at[index],
            device_id=device, device_id_type=MESH,
        )
        copy.start()
        return copy

    sent = fields * HALO
    copies = [
        remote(0, send_rows.at[0, pl.ds(0, sent)], recv_rows.at[0, pl.ds(0, sent)], (core, xp, gy)),
        remote(1, send_rows.at[1, pl.ds(0, sent)], recv_rows.at[1, pl.ds(0, sent)], (core, xn, gy)),
        remote(2, send_cols.at[0], recv_cols.at[0], (core, gx, yp)),
        remote(3, send_cols.at[1], recv_cols.at[1], (core, gx, yn)),
        remote(4, send_corners.at[0], recv_corners.at[0], (core, xp, yp)),
        remote(5, send_corners.at[1], recv_corners.at[1], (core, xp, yn)),
        remote(6, send_corners.at[2], recv_corners.at[2], (core, xn, yp)),
        remote(7, send_corners.at[3], recv_corners.at[3], (core, xn, yn)),
    ]

    count = group_ref.shape[0]
    included = (group_ref[...].reshape(1, count) < 2).astype(F32)
    weights = weight_ref[...].reshape(1, count)
    weight_total = jnp.sum(weights * included, axis=1, keepdims=True)
    row8 = lax.broadcasted_iota(jnp.int32, (SUBLANES, LANES), 0)
    blocks = count // LANES
    pieces = [included[:, b * LANES : (b + 1) * LANES] for b in range(blocks)]
    stacked = jnp.zeros((SUBLANES, LANES), F32)
    for b in range(blocks):
        stacked = jnp.where(row8 == b, jnp.broadcast_to(pieces[b], (SUBLANES, LANES)), stacked)
    before = lax.broadcasted_iota(jnp.int32, (LANES, LANES), 0) <= lax.broadcasted_iota(jnp.int32, (LANES, LANES), 1)
    within = nn(stacked.astype(BF16), before.astype(F32).astype(BF16))
    totals = jnp.sum(stacked, axis=1, keepdims=True)
    slot = (lax.broadcasted_iota(jnp.int32, (SLOTS, LANES), 0) + (core * SLOTS + 1)).astype(F32)
    offset = jnp.zeros((1, 1), F32)
    chosen = []
    for b in range(blocks):
        order = within[b : b + 1] + offset
        offset = offset + totals[b : b + 1]
        order = jnp.where(pieces[b] > 0, order, 0.0)
        chosen.append(jnp.where(slot == jnp.broadcast_to(order, (SLOTS, LANES)), 1.0, 0.0).astype(BF16))
    select = jnp.concatenate(chosen, axis=1)
    w_hi, w_mid, w_lo = split3(weights)
    w_rows = lax.broadcasted_iota(jnp.int32, (SUBLANES, count), 0)
    w_stack = jnp.where(w_rows == 0, w_hi, jnp.where(w_rows == 1, w_mid, jnp.where(w_rows == 2, w_lo, 0.0)))
    found = nt(jnp.concatenate([*split3(points_ref[...]), w_stack], axis=0).astype(BF16), select)
    coords = found[0:dims] + found[dims : 2 * dims] + found[2 * dims : 3 * dims]
    held = found[3 * dims : 3 * dims + 1] + found[3 * dims + 1 : 3 * dims + 2] + found[3 * dims + 2 : 3 * dims + 3]
    node_w[...] = jnp.broadcast_to(held, (SUBLANES, SLOTS))

    csc[0:1, :] = jnp.ones((1, SLOTS), F32)
    csc[1 : 1 + dims, :] = coords
    coefficient = csc[...][0:modes]
    rhs_f[...] = jnp.zeros_like(rhs_f)

    def place(group, half, h, field, scale):
        hi, lo = split2(coefficient[:, h * LANES : (h + 1) * LANES] * scale)
        at = field * modes
        lanes = pl.ds(half * LANES, LANES)
        rhs_f[group, pl.ds(at, modes), lanes] = hi
        rhs_f[group, pl.ds(kpad + at, modes), lanes] = lo
        rhs_f[group, pl.ds(2 * kpad + at, modes), lanes] = hi

    for h in range(2):
        for k in range(4):
            place(2 * h + k // 2, k % 2, h, 3, TIME_STEP)
            place(2 * h + k // 2, k % 2, h, 1 + k // 2, (-0.5, 0.5)[k % 2] * TIME_STEP)
        place(4, h, h, 0, 1.0)
    rhs[...] = rhs_f[...].astype(BF16)

    rest = jnp.zeros((SUBLANES, LANES), F32)

    def turned(x):
        hi, lo = split2(x)
        stack = jnp.concatenate([hi, hi, lo, rest], axis=0).astype(BF16)
        return jnp.transpose(stack).astype(F32)

    def turn_rows(quad):
        for k in range(ROWS):
            x = fv[pl.ds(ROWS * quad - HALO + k, kpad, stride=rows), :]
            lnat[lax.rem(quad, 2), pl.ds(k * ring, LANES), :] = turned(x)

    cfs, us = (cf0, cf1), (ua, ub)

    def targets(group):
        if group == 4:
            return [lambda row: us[0].at[row], lambda row: us[1].at[row]]
        return [
            lambda row: cfs[group // 2].at[row, 2 * (group % 2)],
            lambda row: cfs[group // 2].at[row, 2 * (group % 2) + 1],
        ]

    def parameters(quad):
        slot = lax.rem(quad, 2)
        cells = []
        for k in range(ROWS):
            cells += [lnat[slot, pl.ds(k * ring + j, SUBLANES, stride=chunk), :] for j in range(chunk)]
        left[...] = jnp.concatenate(cells, axis=0).astype(BF16)
        for group in range(5):
            found = nn(left[...], rhs[group])
            for half, target in enumerate(targets(group)):
                for k in range(ROWS):
                    piece = found[k * ring : (k + 1) * ring, half * LANES : (half + 1) * LANES]
                    target(ROWS * quad + k)[...] = piece

    for side in range(2):
        recv_rows[side, pl.ds(sent, kpad * HALO - sent), :] = jnp.zeros((kpad * HALO - sent, LANES), F32)
    acc[...] = jnp.zeros_like(acc)

    turn_rows(1)

    @pl.loop(1, quads - 2)
    def _(quad):
        parameters(quad)
        turn_rows(quad + 1)

    parameters(quads - 2)

    for copy in copies:
        copy.wait_recv()

    for side, quad in ((1, 0), (0, quads - 1)):
        for k in range(ROWS):
            x = recv_rows[side, pl.ds(k, kpad, stride=HALO), :]
            lnat[quad % 2, pl.ds(k * ring, LANES), :] = turned(x)
        parameters(quad)

    for t in range(2 * tiles):
        cols_t[pl.ds(t * LANES, LANES), :] = turned(recv_cols[t // tiles, t % tiles])
    corners = [recv_corners[k] for k in range(4)]
    unpacked = []
    for m in range(groups):
        x = jnp.zeros((SUBLANES, LANES), F32)
        for k in range(4):
            x = jnp.where(by_block == k, pltpu.roll(corners[k], block * (k - m) % LANES, 1), x)
        unpacked.append(x)
    cols_t[pl.ds(2 * tiles * LANES, LANES), :] = turned(jnp.concatenate(unpacked, axis=0))

    def column_halo(row, right, left_side):
        halo_l[pl.ds(row * SUBLANES, HALO), :] = cols_t[pl.ds(right, HALO), :]
        halo_l[pl.ds(row * SUBLANES + HALO, HALO), :] = cols_t[pl.ds(left_side, HALO), :]

    for row in range(rows):
        t, g = divmod(row, per_tile)
        column_halo(
            row + HALO,
            t * LANES + HALO * ((g + 1) % per_tile),
            (tiles + t) * LANES + HALO * g,
        )
    corner = 2 * tiles * LANES
    for r in range(HALO):
        column_halo(rows + HALO + r, corner + HALO * r, corner + block + HALO * r)
        column_halo(r, corner + 2 * block + HALO * r, corner + 3 * block + HALO * r)
    edge = (chunk - SUBLANES) * SUBLANES + SUBLANES - 1
    for group in range(5):
        found = nn(halo_l[...].astype(BF16), rhs[group])
        for half, target in enumerate(targets(group)):
            for row in range(ext):
                piece = found[row * SUBLANES : (row + 1) * SUBLANES, half * LANES : (half + 1) * LANES]
                target(row)[pl.ds(edge, SUBLANES, stride=SUBLANES), :] = piece

    tile = [pl.ds(SUBLANES * j, SUBLANES) for j in range(chunk)]

    def advance(step, h, first):
        cf = cfs[h].at[pl.ds(first, ROWS)]
        u = us[h].at[pl.ds(first, ROWS + 1)]
        cells = [kept.at[h]] + [u.at[k] for k in range(ROWS + 1)]

        def column(j):
            return [ref[tile[j], :] for ref in cells]

        column_now = column(0)
        last = [ref[tile[chunk - 1], :] for ref in cells[1:-1]]
        wrap = [column_now[k + 1] - pltpu.roll(last[k], 1, 0) for k in range(ROWS)]
        south = wrap
        for j in range(chunk):
            if j + 1 < chunk:
                column_next = column(j + 1)
                north = [column_next[k + 1] - column_now[k + 1] for k in range(ROWS)]
            else:
                column_next = None
                north = [pltpu.roll(x, SUBLANES - 1, 0) for x in wrap]
            east = [column_now[k + 1] - column_now[k] for k in range(ROWS + 1)]
            for k in range(ROWS):
                c = [cf[k, m, tile[j], :] for m in range(4)]
                new = column_now[k + 1] + (
                    (c[0] * east[k + 1] - c[1] * east[k]) + (c[2] * north[k] - c[3] * south[k])
                )
                if step < 4:
                    u[k, tile[j], :] = new
                    continue
                one = node_w[:, h * LANES : (h + 1) * LANES] * new
                two = one * new
                if h == 0:
                    part[k, 0, tile[j], :] = one
                    part[k, 1, tile[j], :] = two
                else:
                    both[k, 0, tile[j], :] = one + part[k, 0, tile[j], :]
                    both[k, 1, tile[j], :] = two + part[k, 1, tile[j], :]
            kept[h, tile[j], :] = column_now[ROWS]
            column_now, south = column_next, north

    def gather_sums(first):
        masks = [(lane == first + k + m * rows, k, m) for k in range(ROWS) for m in range(2)]
        for j in range(chunk):
            old = acc[tile[j], :]
            for mask, k, m in masks:
                old = jnp.where(mask, jnp.sum(both[k, m, tile[j], :], axis=1, keepdims=True), old)
            acc[tile[j], :] = old

    for step, (start, turns) in {1: (0, quads), 2: (2, quads - 1), 3: (1, quads - 1), 4: (HALO, quads - 2)}.items():
        for h in range(2):
            kept[h] = us[h][max(start - 1, 0)]
        if step == 4:
            both[...] = jnp.zeros_like(both)

        @pl.loop(0, turns)
        def _(turn):
            first = start + ROWS * turn
            if step == 4:
                gather_sums(first - HALO - ROWS)
            for h in range(2):
                advance(step, h, first)

    gather_sums(rows - ROWS)

    for j in range(chunk):
        nat[pl.ds(j, SUBLANES, stride=chunk), :] = acc[tile[j], :]
    mine[...] = jnp.transpose(nat[0:LANES, :])
    swap = remote(8, mine, theirs, (1 - core, gx, gy))
    for copy in copies:
        copy.wait_send()
    swap.wait()
    moments_ref[...] = (mine[...] + theirs[...]) / weight_total


def on_device(mesh, field_modes, node_points, quad_weight, group_of):
    rows, cols = field_modes.shape[2:]
    count, dims = node_points.shape
    modes = dims + 1
    ext = rows + 2 * HALO
    ring = cols + 2 * HALO
    kpad = 40
    tiles = rows * HALO // LANES
    vmem = pl.BlockSpec(memory_space=pltpu.VMEM)
    moments = pl.pallas_call(
        functools.partial(kernel, mesh.shape["gx"], mesh.shape["gy"], rows, dims),
        out_shape=jax.ShapeDtypeStruct((2 * rows, cols), F32),
        in_specs=[pl.BlockSpec(memory_space=pl.ANY), vmem, vmem, vmem],
        out_specs=vmem,
        scratch_shapes=[
            pltpu.VMEM((kpad * rows, LANES), F32),
            pltpu.VMEM((2, kpad * HALO, LANES), F32),
            pltpu.VMEM((2, kpad * HALO, LANES), F32),
            pltpu.VMEM((2, tiles, kpad, LANES), F32),
            pltpu.VMEM((2, tiles, kpad, LANES), F32),
            pltpu.VMEM((4, SUBLANES, LANES), F32),
            pltpu.VMEM((4, SUBLANES, LANES), F32),
            pltpu.VMEM((2, ROWS * ring, LANES), F32),
            pltpu.VMEM((ROWS * ring, LANES), BF16),
            pltpu.VMEM(((2 * tiles + 1) * LANES, LANES), F32),
            pltpu.VMEM((ext * SUBLANES, LANES), F32),
            pltpu.VMEM((5, LANES, 2 * LANES), F32),
            pltpu.VMEM((5, LANES, 2 * LANES), BF16),
            pltpu.VMEM((SUBLANES, SLOTS), F32),
            pltpu.VMEM((2 * SUBLANES, SLOTS), F32),
            pltpu.VMEM((ext, 4, ring, LANES), F32),
            pltpu.VMEM((ext, 4, ring, LANES), F32),
            pltpu.VMEM((ext + 1, ring, LANES), F32),
            pltpu.VMEM((ext + 1, ring, LANES), F32),
            pltpu.VMEM((2, ring, LANES), F32),
            pltpu.VMEM((ROWS, 2, ring, LANES), F32),
            pltpu.VMEM((ROWS, 2, ring, LANES), F32),
            pltpu.VMEM((ring, LANES), F32),
            pltpu.VMEM((ring, LANES), F32),
            pltpu.VMEM((2 * rows, LANES), F32),
            pltpu.VMEM((2 * rows, LANES), F32),
            pltpu.SemaphoreType.DMA,
            pltpu.SemaphoreType.DMA((9,)),
            pltpu.SemaphoreType.DMA((9,)),
        ],
        compiler_params=pltpu.CompilerParams(
            collective_id=0, has_side_effects=True, vmem_limit_bytes=62 * 1024 * 1024
        ),
    )(
        field_modes.reshape(4 * modes * rows, cols),
        node_points.T,
        quad_weight,
        group_of,
    )
    mean_field = moments[:rows]
    return mean_field, moments[rows:] - mean_field * mean_field


def solution(mesh):
    return jax.shard_map(
        functools.partial(on_device, mesh),
        mesh=mesh,
        in_specs=(P(None, None, "gx", "gy"), P(), P(), P()),
        out_specs=(P("gx", "gy"), P("gx", "gy")),
        check_vma=False,
    )
```

time: 63 us -> 41.3 us (0.66)
  Pallas kernels: 54.5 us -> 39 us
  local copies, waits for them, and re-layouts: 5.4 us -> 0 us
  other arithmetic: 2.04 us -> 1.4 us
    pallas_call x1, Pallas kernels: 54.5 us -> 39 us  [on_device(): pl.pallas_call(functools.partial(kernel, mesh.shape['gx'], mesh.shape['gy...]
    reshape x2 -> x0, local copies, waits for them, and re-layouts: 2.53 us -> none  [the longest x1 1.27 us: on_device(): quad_weight.reshape(1, count)]
    unnamed x1 -> x0, local copies, waits for them, and re-layouts: 1.65 us -> none
    slice x1 -> x0, local copies, waits for them, and re-layouts: 1.22 us -> none  [on_device(): weight_total = wsum[0, 0]]
    sub x1, other arithmetic: 2.04 us -> 1.4 us  [on_device(): return (mean_field, moments[rows:] - mean_field * mean_field)]
where the time goes in v1:
time: 41.3 us; the launch traced here: 41 us
  Pallas kernels  39 us (94%)
  other arithmetic  1.4 us (3%)
  between operations  0.64 us (2%)
    pallas_call x1, Pallas kernels, on_device(): pl.pallas_call(functools.partial(kernel, mesh.shape['gx'], mesh.shape['gy...  39 us
    sub x1, other arithmetic, on_device(): return (mean_field, moments[rows:] - mean_field * mean_field)  1.4 us

profile of v1, /device:TPU:1, one launch (start us, length us, event | category | flops | bytes accessed | tf_op | source)
XLA Modules:
  0.0 41.0 jit_solution(15947554554574534294)
XLA Ops:
  0.6 39.0 %shard_map.59 = f32[128,128]{1,0:T(8,128)} custom-call(f32[2304,128]{1,0:T(8,128)} %bitcast.2, f32[8,768]{1,0:T(8,128)} %bitcast.3, f32[768]{0:T(1024)} %weight_ref.1, s32[768]{0:T(1024)} %group_ref.1), custom_call_target="tpu_custom_call" | custom-call | tf_op jit(solution)/shard_map/pallas_call | solution.py:358
  39.6 1.4 %multiply_subtract_fusion = (f32[64,128]{1,0:T(8,128)}, f32[64,128]{1,0:T(8,128)}) fusion(f32[128,128]{1,0:T(8,128)} %shard_map.59), kind=kLoop, calls=%fused_computation | loop fusion | flops 16384 | bytes 131072 | tf_op jit(solution)/shard_map/sub | solution.py:404

commit v2 on v1

--- a/solution.py
+++ b/solution.py
@@ -40,11 +40,12 @@
 
 def kernel(
     gx_size, gy_size, rows, dims,
-    field_hbm, points_ref, weight_ref, group_ref,
+    field_hbm, points_hbm, weight_hbm, group_hbm,
     moments_ref,
     fv, send_rows, recv_rows, send_cols, recv_cols, send_corners, recv_corners,
     lnat, left, cols_t, halo_l, rhs_f, rhs, node_w, csc,
     cf0, cf1, ua, ub, kept, part, both, acc, nat, mine, theirs,
+    points_ref, weight_ref, group_ref,
     load_sem, send_sem, recv_sem,
 ):
     ext = rows + 2 * HALO
@@ -66,18 +67,49 @@
         (1 - core, gx, gy),
     ]
 
-    load = pltpu.make_async_copy(field_hbm, fv.at[pl.ds(0, fields * rows)], load_sem)
-    load.start()
     barrier = pltpu.get_barrier_semaphore()
     for device in around:
         pl.semaphore_signal(barrier, inc=1, device_id=device, device_id_type=MESH)
 
-    fv[pl.ds(fields * rows, (kpad - fields) * rows), :] = jnp.zeros(((kpad - fields) * rows, LANES), F32)
-    load.wait()
+    apart = fv.shape[0] // kpad
+
+    @pl.loop(0, fields)
+    def _(k):
+        pltpu.make_async_copy(
+            field_hbm.at[pl.ds(k * rows, rows)], fv.at[pl.ds(k * apart, rows)], load_sem.at[0]
+        ).start()
+
+    small = [
+        pltpu.make_async_copy(source, target, load_sem.at[1 + i])
+        for i, (source, target) in enumerate(
+            [(points_hbm, points_ref), (weight_hbm, weight_ref), (group_hbm, group_ref)]
+        )
+    ]
+    for copy in small:
+        copy.start()
+    fv[pl.ds(fields * apart, (kpad - fields) * apart), :] = jnp.zeros(((kpad - fields) * apart, LANES), F32)
+    pltpu.make_async_copy(field_hbm, fv.at[pl.ds(0, fields * rows)], load_sem.at[0]).wait()
 
     for r in range(HALO):
-        send_rows[0, pl.ds(r, kpad, stride=HALO), :] = fv[pl.ds(r, kpad, stride=rows), :]
-        send_rows[1, pl.ds(r, kpad, stride=HALO), :] = fv[pl.ds(rows - HALO + r, kpad, stride=rows), :]
+        send_rows[0, pl.ds(r, kpad, stride=HALO), :] = fv[pl.ds(r, kpad, stride=apart), :]
+        send_rows[1, pl.ds(r, kpad, stride=HALO), :] = fv[pl.ds(rows - HALO + r, kpad, stride=apart), :]
+
+    pl.semaphore_wait(barrier, len(around))
+
+    def remote(index, source, target, device):
+        copy = pltpu.make_async_remote_copy(
+            src_ref=source, dst_ref=target,
+            send_sem=send_sem.at[index], recv_sem=recv_sem.at[index],
+            device_id=device, device_id_type=MESH,
+        )
+        copy.start()
+        return copy
+
+    sent = fields * HALO
+    copies = [
+        remote(0, send_rows.at[0, pl.ds(0, sent)], recv_rows.at[0, pl.ds(0, sent)], (core, xp, gy)),
+        remote(1, send_rows.at[1, pl.ds(0, sent)], recv_rows.at[1, pl.ds(0, sent)], (core, xn, gy)),
+    ]
     lane = lax.broadcasted_iota(jnp.int32, (SUBLANES, LANES), 1)
     by_halo = lane // HALO
     block = HALO * HALO
@@ -91,7 +123,7 @@
             at_high = by_halo == g
             at_low = by_halo == (g + 1) % per_tile
             for m in range(groups):
-                x = fv[pl.ds(m * SUBLANES * rows + t * per_tile + g, SUBLANES, stride=rows), :]
+                x = fv[pl.ds(m * SUBLANES * apart + t * per_tile + g, SUBLANES, stride=apart), :]
                 x = pltpu.roll(x, (HALO * (g + 1)) % LANES, 1)
                 high[m] = jnp.where(at_high, x, high[m])
                 low[m] = jnp.where(at_low, x, low[m])
@@ -107,21 +139,7 @@
                     packed = jnp.where(by_block == m, pltpu.roll(values[m], (block * m - at) % LANES, 1), packed)
                 send_corners[2 * end + side] = packed
 
-    pl.semaphore_wait(barrier, len(around))
-
-    def remote(index, source, target, device):
-        copy = pltpu.make_async_remote_copy(
-            src_ref=source, dst_ref=target,
-            send_sem=send_sem.at[index], recv_sem=recv_sem.at[index],
-            device_id=device, device_id_type=MESH,
-        )
-        copy.start()
-        return copy
-
-    sent = fields * HALO
-    copies = [
-        remote(0, send_rows.at[0, pl.ds(0, sent)], recv_rows.at[0, pl.ds(0, sent)], (core, xp, gy)),
-        remote(1, send_rows.at[1, pl.ds(0, sent)], recv_rows.at[1, pl.ds(0, sent)], (core, xn, gy)),
+    copies += [
         remote(2, send_cols.at[0], recv_cols.at[0], (core, gx, yp)),
         remote(3, send_cols.at[1], recv_cols.at[1], (core, gx, yn)),
         remote(4, send_corners.at[0], recv_corners.at[0], (core, xp, yp)),
@@ -130,6 +148,8 @@
         remote(7, send_corners.at[3], recv_corners.at[3], (core, xn, yn)),
     ]
 
+    for copy in small:
+        copy.wait()
     count = group_ref.shape[0]
     included = (group_ref[...].reshape(1, count) < 2).astype(F32)
     weights = weight_ref[...].reshape(1, count)
@@ -189,7 +209,7 @@
 
     def turn_rows(quad):
         for k in range(ROWS):
-            x = fv[pl.ds(ROWS * quad - HALO + k, kpad, stride=rows), :]
+            x = fv[pl.ds(ROWS * quad - HALO + k, kpad, stride=apart), :]
             lnat[lax.rem(quad, 2), pl.ds(k * ring, LANES), :] = turned(x)
 
     cfs, us = (cf0, cf1), (ua, ub)
@@ -358,10 +378,10 @@
     moments = pl.pallas_call(
         functools.partial(kernel, mesh.shape["gx"], mesh.shape["gy"], rows, dims),
         out_shape=jax.ShapeDtypeStruct((2 * rows, cols), F32),
-        in_specs=[pl.BlockSpec(memory_space=pl.ANY), vmem, vmem, vmem],
+        in_specs=[pl.BlockSpec(memory_space=pl.ANY)] * 4,
         out_specs=vmem,
         scratch_shapes=[
-            pltpu.VMEM((kpad * rows, LANES), F32),
+            pltpu.VMEM((kpad * (rows + SUBLANES), LANES), F32),
             pltpu.VMEM((2, kpad * HALO, LANES), F32),
             pltpu.VMEM((2, kpad * HALO, LANES), F32),
             pltpu.VMEM((2, tiles, kpad, LANES), F32),
@@ -387,7 +407,10 @@
             pltpu.VMEM((ring, LANES), F32),
             pltpu.VMEM((2 * rows, LANES), F32),
             pltpu.VMEM((2 * rows, LANES), F32),
-            pltpu.SemaphoreType.DMA,
+            pltpu.VMEM((dims, count), F32),
+            pltpu.VMEM((count,), F32),
+            pltpu.VMEM((count,), jnp.int32),
+            pltpu.SemaphoreType.DMA((4,)),
             pltpu.SemaphoreType.DMA((9,)),
             pltpu.SemaphoreType.DMA((9,)),
         ],

time: 41.3 us -> 41.2 us (level)
  no operation moved by 1% of the time
where the time goes in v2:
time: 41.2 us; the launch traced here: 40.9 us
  Pallas kernels  38.9 us (94%)
  other arithmetic  1.4 us (3%)
  between operations  0.64 us (2%)
    pallas_call x1, Pallas kernels, on_device(): pl.pallas_call(functools.partial(kernel, mesh.shape['gx'], mesh.shape['gy...  38.9 us
    sub x1, other arithmetic, on_device(): return (mean_field, moments[rows:] - mean_field * mean_field)  1.4 us

profile of v2, /device:TPU:1, one launch (start us, length us, event | category | flops | bytes accessed | tf_op | source)
XLA Modules:
  0.0 40.9 jit_solution(2270490728552298126)
XLA Ops:
  0.6 38.9 %shard_map.59 = f32[128,128]{1,0:T(8,128)} custom-call(f32[2304,128]{1,0:T(8,128)} %bitcast.2, f32[8,768]{1,0:T(8,128)} %bitcast.3, f32[768]{0:T(1024)} %weight_hbm.1, s32[768]{0:T(1024)} %group_hbm.1), custom_call_target="tpu_custom_call" | custom-call | tf_op jit(solution)/shard_map/pallas_call | solution.py:378
  39.5 1.4 %multiply_subtract_fusion = (f32[64,128]{1,0:T(8,128)}, f32[64,128]{1,0:T(8,128)}) fusion(f32[128,128]{1,0:T(8,128)} %shard_map.59), kind=kLoop, calls=%fused_computation | loop fusion | flops 16384 | bytes 131072 | tf_op jit(solution)/shard_map/sub | solution.py:427

commit v3 on v2

--- a/solution.py
+++ b/solution.py
@@ -13,6 +13,7 @@
 SUBLANES = 8
 SLOTS = 256
 ROWS = 4
+EARLY = 4
 MESH = pl.DeviceIdType.MESH
 F32 = jnp.float32
 BF16 = jnp.bfloat16
@@ -88,65 +89,6 @@
     for copy in small:
         copy.start()
     fv[pl.ds(fields * apart, (kpad - fields) * apart), :] = jnp.zeros(((kpad - fields) * apart, LANES), F32)
-    pltpu.make_async_copy(field_hbm, fv.at[pl.ds(0, fields * rows)], load_sem.at[0]).wait()
-
-    for r in range(HALO):
-        send_rows[0, pl.ds(r, kpad, stride=HALO), :] = fv[pl.ds(r, kpad, stride=apart), :]
-        send_rows[1, pl.ds(r, kpad, stride=HALO), :] = fv[pl.ds(rows - HALO + r, kpad, stride=apart), :]
-
-    pl.semaphore_wait(barrier, len(around))
-
-    def remote(index, source, target, device):
-        copy = pltpu.make_async_remote_copy(
-            src_ref=source, dst_ref=target,
-            send_sem=send_sem.at[index], recv_sem=recv_sem.at[index],
-            device_id=device, device_id_type=MESH,
-        )
-        copy.start()
-        return copy
-
-    sent = fields * HALO
-    copies = [
-        remote(0, send_rows.at[0, pl.ds(0, sent)], recv_rows.at[0, pl.ds(0, sent)], (core, xp, gy)),
-        remote(1, send_rows.at[1, pl.ds(0, sent)], recv_rows.at[1, pl.ds(0, sent)], (core, xn, gy)),
-    ]
-    lane = lax.broadcasted_iota(jnp.int32, (SUBLANES, LANES), 1)
-    by_halo = lane // HALO
-    block = HALO * HALO
-    by_block = lane // block
-    per_tile = LANES // HALO
-    tiles = rows // per_tile
-    for t in range(tiles):
-        low = [jnp.zeros((SUBLANES, LANES), F32)] * groups
-        high = [jnp.zeros((SUBLANES, LANES), F32)] * groups
-        for g in range(per_tile):
-            at_high = by_halo == g
-            at_low = by_halo == (g + 1) % per_tile
-            for m in range(groups):
-                x = fv[pl.ds(m * SUBLANES * apart + t * per_tile + g, SUBLANES, stride=apart), :]
-                x = pltpu.roll(x, (HALO * (g + 1)) % LANES, 1)
-                high[m] = jnp.where(at_high, x, high[m])
-                low[m] = jnp.where(at_low, x, low[m])
-        for side, values in enumerate((low, high)):
-            for m in range(groups):
-                send_cols[side, t, m * SUBLANES : (m + 1) * SUBLANES, :] = values[m]
-            for end in range(2):
-                if t != (0, tiles - 1)[end]:
-                    continue
-                at = HALO * (1 - side) + (0, LANES - block)[end]
-                packed = jnp.zeros((SUBLANES, LANES), F32)
-                for m in range(groups):
-                    packed = jnp.where(by_block == m, pltpu.roll(values[m], (block * m - at) % LANES, 1), packed)
-                send_corners[2 * end + side] = packed
-
-    copies += [
-        remote(2, send_cols.at[0], recv_cols.at[0], (core, gx, yp)),
-        remote(3, send_cols.at[1], recv_cols.at[1], (core, gx, yn)),
-        remote(4, send_corners.at[0], recv_corners.at[0], (core, xp, yp)),
-        remote(5, send_corners.at[1], recv_corners.at[1], (core, xp, yn)),
-        remote(6, send_corners.at[2], recv_corners.at[2], (core, xn, yp)),
-        remote(7, send_corners.at[3], recv_corners.at[3], (core, xn, yn)),
-    ]
 
     for copy in small:
         copy.wait()
@@ -235,13 +177,75 @@
                     piece = found[k * ring : (k + 1) * ring, half * LANES : (half + 1) * LANES]
                     target(ROWS * quad + k)[...] = piece
 
+    sent = fields * HALO
     for side in range(2):
         recv_rows[side, pl.ds(sent, kpad * HALO - sent), :] = jnp.zeros((kpad * HALO - sent, LANES), F32)
     acc[...] = jnp.zeros_like(acc)
+    pltpu.make_async_copy(field_hbm, fv.at[pl.ds(0, fields * rows)], load_sem.at[0]).wait()
+
+    lane = lax.broadcasted_iota(jnp.int32, (SUBLANES, LANES), 1)
+    by_halo = lane // HALO
+    block = HALO * HALO
+    by_block = lane // block
+    per_tile = LANES // HALO
+    tiles = rows // per_tile
+
+    for r in range(HALO):
+        send_rows[0, pl.ds(r, kpad, stride=HALO), :] = fv[pl.ds(r, kpad, stride=apart), :]
+        send_rows[1, pl.ds(r, kpad, stride=HALO), :] = fv[pl.ds(rows - HALO + r, kpad, stride=apart), :]
+    for t in range(tiles):
+        low = [jnp.zeros((SUBLANES, LANES), F32)] * groups
+        high = [jnp.zeros((SUBLANES, LANES), F32)] * groups
+        for g in range(per_tile):
+            at_high = by_halo == g
+            at_low = by_halo == (g + 1) % per_tile
+            for m in range(groups):
+                x = fv[pl.ds(m * SUBLANES * apart + t * per_tile + g, SUBLANES, stride=apart), :]
+                x = pltpu.roll(x, (HALO * (g + 1)) % LANES, 1)
+                high[m] = jnp.where(at_high, x, high[m])
+                low[m] = jnp.where(at_low, x, low[m])
+        for side, values in enumerate((low, high)):
+            for m in range(groups):
+                send_cols[side, t, m * SUBLANES : (m + 1) * SUBLANES, :] = values[m]
+            for end in range(2):
+                if t != (0, tiles - 1)[end]:
+                    continue
+                at = HALO * (1 - side) + (0, LANES - block)[end]
+                packed = jnp.zeros((SUBLANES, LANES), F32)
+                for m in range(groups):
+                    packed = jnp.where(by_block == m, pltpu.roll(values[m], (block * m - at) % LANES, 1), packed)
+                send_corners[2 * end + side] = packed
 
     turn_rows(1)
 
-    @pl.loop(1, quads - 2)
+    @pl.loop(1, 1 + EARLY)
+    def _(quad):
+        parameters(quad)
+        turn_rows(quad + 1)
+
+    pl.semaphore_wait(barrier, len(around))
+
+    def remote(index, source, target, device):
+        copy = pltpu.make_async_remote_copy(
+            src_ref=source, dst_ref=target,
+            send_sem=send_sem.at[index], recv_sem=recv_sem.at[index],
+            device_id=device, device_id_type=MESH,
+        )
+        copy.start()
+        return copy
+
+    copies = [
+        remote(0, send_rows.at[0, pl.ds(0, sent)], recv_rows.at[0, pl.ds(0, sent)], (core, xp, gy)),
+        remote(1, send_rows.at[1, pl.ds(0, sent)], recv_rows.at[1, pl.ds(0, sent)], (core, xn, gy)),
+        remote(2, send_cols.at[0], recv_cols.at[0], (core, gx, yp)),
+        remote(3, send_cols.at[1], recv_cols.at[1], (core, gx, yn)),
+        remote(4, send_corners.at[0], recv_corners.at[0], (core, xp, yp)),
+        remote(5, send_corners.at[1], recv_corners.at[1], (core, xp, yn)),
+        remote(6, send_corners.at[2], recv_corners.at[2], (core, xn, yp)),
+        remote(7, send_corners.at[3], recv_corners.at[3], (core, xn, yn)),
+    ]
+
+    @pl.loop(1 + EARLY, quads - 2)
     def _(quad):
         parameters(quad)
         turn_rows(quad + 1)
@@ -377,7 +381,7 @@
     vmem = pl.BlockSpec(memory_space=pltpu.VMEM)
     moments = pl.pallas_call(
         functools.partial(kernel, mesh.shape["gx"], mesh.shape["gy"], rows, dims),
-        out_shape=jax.ShapeDtypeStruct((2 * rows, cols), F32),
+        out_shape=pltpu.VMEM((2 * rows, cols), F32),
         in_specs=[pl.BlockSpec(memory_space=pl.ANY)] * 4,
         out_specs=vmem,
         scratch_shapes=[

time: 41.2 us -> 36.9 us (0.90)
  Pallas kernels: 38.9 us -> 35.4 us
  other arithmetic: 1.4 us -> 0.63 us
    pallas_call x1, Pallas kernels: 38.9 us -> 35.4 us  [on_device(): pl.pallas_call(functools.partial(kernel, mesh.shape['gx'], mesh.shape['gy...]
    sub x1, other arithmetic: 1.4 us -> 0.63 us  [on_device(): return (mean_field, moments[rows:] - mean_field * mean_field)]
where the time goes in v3:
time: 36.9 us; the launch traced here: 36.7 us
  Pallas kernels  35.4 us (96%)
  between operations  0.64 us (2%)
  other arithmetic  0.63 us (2%)
    pallas_call x1, Pallas kernels, on_device(): pl.pallas_call(functools.partial(kernel, mesh.shape['gx'], mesh.shape['gy...  35.4 us

profile of v3, /device:TPU:1, one launch (start us, length us, event | category | flops | bytes accessed | tf_op | source)
XLA Modules:
  0.0 36.7 jit_solution(14208496393931864008)
XLA Ops:
  0.6 35.4 %shard_map.59 = f32[128,128]{1,0:T(8,128)S(1)} custom-call(f32[2304,128]{1,0:T(8,128)} %bitcast.2, f32[8,768]{1,0:T(8,128)} %bitcast.3, f32[768]{0:T(1024)} %weight_hbm.1, s32[768]{0:T(1024)} %group_hbm.1), custom_call_target="tpu_custom_call" | custom-call | tf_op jit(solution)/shard_map/pallas_call | solution.py:382
  36.1 0.6 %multiply_subtract_fusion = (f32[64,128]{1,0:T(8,128)}, f32[64,128]{1,0:T(8,128)}) fusion(f32[128,128]{1,0:T(8,128)S(1)} %shard_map.59), kind=kLoop, calls=%fused_computation | loop fusion | flops 16384 | bytes 131072 | tf_op jit(solution)/shard_map/sub | solution.py:431

commit v4 on v3

--- a/solution.py
+++ b/solution.py
@@ -235,14 +235,14 @@
         return copy
 
     copies = [
+        remote(4, send_corners.at[0], recv_corners.at[0], (core, xp, yp)),
+        remote(5, send_corners.at[1], recv_corners.at[1], (core, xp, yn)),
+        remote(6, send_corners.at[2], recv_corners.at[2], (core, xn, yp)),
+        remote(7, send_corners.at[3], recv_corners.at[3], (core, xn, yn)),
         remote(0, send_rows.at[0, pl.ds(0, sent)], recv_rows.at[0, pl.ds(0, sent)], (core, xp, gy)),
         remote(1, send_rows.at[1, pl.ds(0, sent)], recv_rows.at[1, pl.ds(0, sent)], (core, xn, gy)),
         remote(2, send_cols.at[0], recv_cols.at[0], (core, gx, yp)),
         remote(3, send_cols.at[1], recv_cols.at[1], (core, gx, yn)),
-        remote(4, send_corners.at[0], recv_corners.at[0], (core, xp, yp)),
-        remote(5, send_corners.at[1], recv_corners.at[1], (core, xp, yn)),
-        remote(6, send_corners.at[2], recv_corners.at[2], (core, xn, yp)),
-        remote(7, send_corners.at[3], recv_corners.at[3], (core, xn, yn)),
     ]
 
     @pl.loop(1 + EARLY, quads - 2)

time: 36.9 us -> 36.5 us (0.989)
    pallas_call x1, Pallas kernels: 35.4 us -> 35.1 us  [on_device(): pl.pallas_call(functools.partial(kernel, mesh.shape['gx'], mesh.shape['gy...]
where the time goes in v4:
time: 36.5 us; the launch traced here: 36.3 us
  Pallas kernels  35.1 us (96%)
  between operations  0.64 us (2%)
  other arithmetic  0.63 us (2%)
    pallas_call x1, Pallas kernels, on_device(): pl.pallas_call(functools.partial(kernel, mesh.shape['gx'], mesh.shape['gy...  35.1 us

profile of v4, /device:TPU:1, one launch (start us, length us, event | category | flops | bytes accessed | tf_op | source)
XLA Modules:
  0.0 36.3 jit_solution(8209098550281082522)
XLA Ops:
  0.6 35.1 %shard_map.59 = f32[128,128]{1,0:T(8,128)S(1)} custom-call(f32[2304,128]{1,0:T(8,128)} %bitcast.2, f32[8,768]{1,0:T(8,128)} %bitcast.3, f32[768]{0:T(1024)} %weight_hbm.1, s32[768]{0:T(1024)} %group_hbm.1), custom_call_target="tpu_custom_call" | custom-call | tf_op jit(solution)/shard_map/pallas_call | solution.py:382
  35.7 0.6 %multiply_subtract_fusion = (f32[64,128]{1,0:T(8,128)}, f32[64,128]{1,0:T(8,128)}) fusion(f32[128,128]{1,0:T(8,128)S(1)} %shard_map.59), kind=kLoop, calls=%fused_computation | loop fusion | flops 16384 | bytes 131072 | tf_op jit(solution)/shard_map/sub | solution.py:431

commit v5 on v4

--- a/solution.py
+++ b/solution.py
@@ -45,7 +45,7 @@
     moments_ref,
     fv, send_rows, recv_rows, send_cols, recv_cols, send_corners, recv_corners,
     lnat, left, cols_t, halo_l, rhs_f, rhs, node_w, csc,
-    cf0, cf1, ua, ub, kept, part, both, acc, nat, mine, theirs,
+    cells0, cells1, kept, aside, part, both, acc, nat, mine, theirs,
     points_ref, weight_ref, group_ref,
     load_sem, send_sem, recv_sem,
 ):
@@ -64,7 +64,6 @@
     yn, yp = lax.rem(gy + 1, gy_size), lax.rem(gy + gy_size - 1, gy_size)
     around = [
         (core, xp, gy), (core, xn, gy), (core, gx, yp), (core, gx, yn),
-        (core, xp, yp), (core, xp, yn), (core, xn, yp), (core, xn, yn),
         (1 - core, gx, gy),
     ]
 
@@ -138,7 +137,7 @@
     for h in range(2):
         for k in range(4):
             place(2 * h + k // 2, k % 2, h, 3, TIME_STEP)
-            place(2 * h + k // 2, k % 2, h, 1 + k // 2, (-0.5, 0.5)[k % 2] * TIME_STEP)
+            place(2 * h + k // 2, k % 2, h, 1 + k // 2, (0.5, -0.5, -0.5, 0.5)[k] * TIME_STEP)
         place(4, h, h, 0, 1.0)
     rhs[...] = rhs_f[...].astype(BF16)
 
@@ -149,19 +148,21 @@
         stack = jnp.concatenate([hi, hi, lo, rest], axis=0).astype(BF16)
         return jnp.transpose(stack).astype(F32)
 
+    top = rows + HALO - 1
+
     def turn_rows(quad):
         for k in range(ROWS):
-            x = fv[pl.ds(ROWS * quad - HALO + k, kpad, stride=apart), :]
+            x = fv[pl.ds(top - ROWS * quad - k, kpad, stride=apart), :]
             lnat[lax.rem(quad, 2), pl.ds(k * ring, LANES), :] = turned(x)
 
-    cfs, us = (cf0, cf1), (ua, ub)
+    planes = (cells0, cells1)
 
     def targets(group):
         if group == 4:
-            return [lambda row: us[0].at[row], lambda row: us[1].at[row]]
+            return [lambda row: planes[0].at[row, 4], lambda row: planes[1].at[row, 4]]
         return [
-            lambda row: cfs[group // 2].at[row, 2 * (group % 2)],
-            lambda row: cfs[group // 2].at[row, 2 * (group % 2) + 1],
+            lambda row: planes[group // 2].at[row, 2 * (group % 2)],
+            lambda row: planes[group // 2].at[row, 2 * (group % 2) + 1],
         ]
 
     def parameters(quad):
@@ -207,14 +208,6 @@
         for side, values in enumerate((low, high)):
             for m in range(groups):
                 send_cols[side, t, m * SUBLANES : (m + 1) * SUBLANES, :] = values[m]
-            for end in range(2):
-                if t != (0, tiles - 1)[end]:
-                    continue
-                at = HALO * (1 - side) + (0, LANES - block)[end]
-                packed = jnp.zeros((SUBLANES, LANES), F32)
-                for m in range(groups):
-                    packed = jnp.where(by_block == m, pltpu.roll(values[m], (block * m - at) % LANES, 1), packed)
-                send_corners[2 * end + side] = packed
 
     turn_rows(1)
 
@@ -235,14 +228,10 @@
         return copy
 
     copies = [
-        remote(4, send_corners.at[0], recv_corners.at[0], (core, xp, yp)),
-        remote(5, send_corners.at[1], recv_corners.at[1], (core, xp, yn)),
-        remote(6, send_corners.at[2], recv_corners.at[2], (core, xn, yp)),
-        remote(7, send_corners.at[3], recv_corners.at[3], (core, xn, yn)),
+        remote(2, send_cols.at[0], recv_cols.at[0], (core, gx, yp)),
+        remote(3, send_cols.at[1], recv_cols.at[1], (core, gx, yn)),
         remote(0, send_rows.at[0, pl.ds(0, sent)], recv_rows.at[0, pl.ds(0, sent)], (core, xp, gy)),
         remote(1, send_rows.at[1, pl.ds(0, sent)], recv_rows.at[1, pl.ds(0, sent)], (core, xn, gy)),
-        remote(2, send_cols.at[0], recv_cols.at[0], (core, gx, yp)),
-        remote(3, send_cols.at[1], recv_cols.at[1], (core, gx, yn)),
     ]
 
     @pl.loop(1 + EARLY, quads - 2)
@@ -252,55 +241,83 @@
 
     parameters(quads - 2)
 
-    for copy in copies:
-        copy.wait_recv()
-
-    for side, quad in ((1, 0), (0, quads - 1)):
+    edge = (chunk - SUBLANES) * SUBLANES + SUBLANES - 1
+
+    def halo_rows(side, quad):
         for k in range(ROWS):
-            x = recv_rows[side, pl.ds(k, kpad, stride=HALO), :]
+            row = top - (ROWS * quad + k)
+            x = recv_rows[side, pl.ds(row - rows if side == 0 else row + HALO, kpad, stride=HALO), :]
             lnat[quad % 2, pl.ds(k * ring, LANES), :] = turned(x)
         parameters(quad)
 
+    def fill(e, right, left_side):
+        halo_l[pl.ds(e * SUBLANES, HALO), :] = cols_t[pl.ds(right, HALO), :]
+        halo_l[pl.ds(e * SUBLANES + HALO, HALO), :] = cols_t[pl.ds(left_side, HALO), :]
+
+    def patch(first, number):
+        cells = halo_l[pl.ds(first * SUBLANES, number * SUBLANES), :].astype(BF16)
+        for group in range(5):
+            found = nn(cells, rhs[group])
+            for half, target in enumerate(targets(group)):
+                for k in range(number):
+                    piece = found[k * SUBLANES : (k + 1) * SUBLANES, half * LANES : (half + 1) * LANES]
+                    target(first + k)[pl.ds(edge, SUBLANES, stride=SUBLANES), :] = piece
+
+    for copy in copies[:2]:
+        copy.wait_recv()
     for t in range(2 * tiles):
         cols_t[pl.ds(t * LANES, LANES), :] = turned(recv_cols[t // tiles, t % tiles])
-    corners = [recv_corners[k] for k in range(4)]
-    unpacked = []
-    for m in range(groups):
-        x = jnp.zeros((SUBLANES, LANES), F32)
-        for k in range(4):
-            x = jnp.where(by_block == k, pltpu.roll(corners[k], block * (k - m) % LANES, 1), x)
-        unpacked.append(x)
-    cols_t[pl.ds(2 * tiles * LANES, LANES), :] = turned(jnp.concatenate(unpacked, axis=0))
-
-    def column_halo(row, right, left_side):
-        halo_l[pl.ds(row * SUBLANES, HALO), :] = cols_t[pl.ds(right, HALO), :]
-        halo_l[pl.ds(row * SUBLANES + HALO, HALO), :] = cols_t[pl.ds(left_side, HALO), :]
-
     for row in range(rows):
         t, g = divmod(row, per_tile)
-        column_halo(
-            row + HALO,
-            t * LANES + HALO * ((g + 1) % per_tile),
-            (tiles + t) * LANES + HALO * g,
-        )
-    corner = 2 * tiles * LANES
-    for r in range(HALO):
-        column_halo(rows + HALO + r, corner + HALO * r, corner + block + HALO * r)
-        column_halo(r, corner + 2 * block + HALO * r, corner + 3 * block + HALO * r)
-    edge = (chunk - SUBLANES) * SUBLANES + SUBLANES - 1
-    for group in range(5):
-        found = nn(halo_l[...].astype(BF16), rhs[group])
-        for half, target in enumerate(targets(group)):
-            for row in range(ext):
-                piece = found[row * SUBLANES : (row + 1) * SUBLANES, half * LANES : (half + 1) * LANES]
-                target(row)[pl.ds(edge, SUBLANES, stride=SUBLANES), :] = piece
+        fill(top - row, t * LANES + HALO * ((g + 1) % per_tile), (tiles + t) * LANES + HALO * g)
+    patch(HALO, rows)
+
+    for copy in copies[2:]:
+        copy.wait_recv()
+    for side in range(2):
+        low = jnp.zeros((SUBLANES, LANES), F32)
+        high = jnp.zeros((SUBLANES, LANES), F32)
+        for m in range(groups):
+            for r in range(HALO):
+                x = recv_rows[side, pl.ds(m * SUBLANES * HALO + r, SUBLANES, stride=HALO), :]
+                at = block * m + HALO * r
+                mask = by_halo == at // HALO
+                low = jnp.where(mask, pltpu.roll(x, at, 1) if at else x, low)
+                high = jnp.where(mask, pltpu.roll(x, at + HALO, 1), high)
+        send_corners[2 * side] = low
+        send_corners[2 * side + 1] = high
+    corner_copies = [
+        remote(4, send_corners.at[0], recv_corners.at[0], (core, gx, yp)),
+        remote(5, send_corners.at[1], recv_corners.at[1], (core, gx, yn)),
+        remote(6, send_corners.at[2], recv_corners.at[2], (core, gx, yp)),
+        remote(7, send_corners.at[3], recv_corners.at[3], (core, gx, yn)),
+    ]
+
+    def halo_ends():
+        halo_rows(0, 0)
+        halo_rows(1, quads - 1)
+        for copy in corner_copies:
+            copy.wait_recv()
+        corners = [recv_corners[k] for k in range(4)]
+        unpacked = []
+        for m in range(groups):
+            x = jnp.zeros((SUBLANES, LANES), F32)
+            for k in range(4):
+                x = jnp.where(by_block == k, pltpu.roll(corners[k], block * (k - m) % LANES, 1), x)
+            unpacked.append(x)
+        corner = 2 * tiles * LANES
+        cols_t[pl.ds(corner, LANES), :] = turned(jnp.concatenate(unpacked, axis=0))
+        for r in range(HALO):
+            fill(top - rows - r, corner + HALO * r, corner + block + HALO * r)
+            fill(top + HALO - r, corner + 2 * block + HALO * r, corner + 3 * block + HALO * r)
+        patch(0, HALO)
+        patch(ext - HALO, HALO)
 
     tile = [pl.ds(SUBLANES * j, SUBLANES) for j in range(chunk)]
 
-    def advance(step, h, first):
-        cf = cfs[h].at[pl.ds(first, ROWS)]
-        u = us[h].at[pl.ds(first, ROWS + 1)]
-        cells = [kept.at[h]] + [u.at[k] for k in range(ROWS + 1)]
+    def advance(step, h, plane, skip, beyond=None):
+        cells = [kept.at[h]] + [plane.at[skip + k, 4] for k in range(ROWS)]
+        cells.append(plane.at[skip + ROWS, 4] if beyond is None else beyond)
 
         def column(j):
             return [ref[tile[j], :] for ref in cells]
@@ -318,12 +335,12 @@
                 north = [pltpu.roll(x, SUBLANES - 1, 0) for x in wrap]
             east = [column_now[k + 1] - column_now[k] for k in range(ROWS + 1)]
             for k in range(ROWS):
-                c = [cf[k, m, tile[j], :] for m in range(4)]
+                c = [plane[skip + k, m, tile[j], :] for m in range(4)]
                 new = column_now[k + 1] + (
                     (c[0] * east[k + 1] - c[1] * east[k]) + (c[2] * north[k] - c[3] * south[k])
                 )
                 if step < 4:
-                    u[k, tile[j], :] = new
+                    plane[skip + k, 4, tile[j], :] = new
                     continue
                 one = node_w[:, h * LANES : (h + 1) * LANES] * new
                 two = one * new
@@ -337,34 +354,48 @@
             column_now, south = column_next, north
 
     def gather_sums(first):
-        masks = [(lane == first + k + m * rows, k, m) for k in range(ROWS) for m in range(2)]
+        masks = [(lane == top - first - k + m * rows, k, m) for k in range(ROWS) for m in range(2)]
         for j in range(chunk):
             old = acc[tile[j], :]
             for mask, k, m in masks:
                 old = jnp.where(mask, jnp.sum(both[k, m, tile[j], :], axis=1, keepdims=True), old)
             acc[tile[j], :] = old
 
-    for step, (start, turns) in {1: (0, quads), 2: (2, quads - 1), 3: (1, quads - 1), 4: (HALO, quads - 2)}.items():
+    inner = HALO + 1
+    spans = {1: (inner, (rows - 2) // ROWS), 2: (2, quads - 1), 3: (1, quads - 1), 4: (HALO, quads - 2)}
+    for step, (start, turns) in spans.items():
         for h in range(2):
-            kept[h] = us[h][max(start - 1, 0)]
+            kept[h] = planes[h][start - 1, 4]
+            if step == 1:
+                aside[h] = planes[h][start, 4]
         if step == 4:
             both[...] = jnp.zeros_like(both)
 
+        def run(first):
+            if step == 4:
+                gather_sums(first - ROWS)
+            for h in range(2):
+                advance(step, h, planes[h].at[pl.ds(first, ROWS + 1)], 0)
+
         @pl.loop(0, turns)
         def _(turn):
-            first = start + ROWS * turn
-            if step == 4:
-                gather_sums(first - HALO - ROWS)
+            run(start + ROWS * turn)
+
+        if step == 1:
+            halo_ends()
+            for first in range(start + ROWS * turns, ext - 1, ROWS):
+                run(first)
             for h in range(2):
-                advance(step, h, first)
-
-    gather_sums(rows - ROWS)
+                kept[h] = planes[h][0, 4]
+                advance(step, h, planes[h].at[pl.ds(1, ROWS + 1)], 0, aside.at[h])
+
+    gather_sums(rows + HALO - ROWS)
 
     for j in range(chunk):
         nat[pl.ds(j, SUBLANES, stride=chunk), :] = acc[tile[j], :]
     mine[...] = jnp.transpose(nat[0:LANES, :])
     swap = remote(8, mine, theirs, (1 - core, gx, gy))
-    for copy in copies:
+    for copy in copies + corner_copies:
         copy.wait_send()
     swap.wait()
     moments_ref[...] = (mine[...] + theirs[...]) / weight_total
@@ -400,10 +431,9 @@
             pltpu.VMEM((5, LANES, 2 * LANES), BF16),
             pltpu.VMEM((SUBLANES, SLOTS), F32),
             pltpu.VMEM((2 * SUBLANES, SLOTS), F32),
-            pltpu.VMEM((ext, 4, ring, LANES), F32),
-            pltpu.VMEM((ext, 4, ring, LANES), F32),
-            pltpu.VMEM((ext + 1, ring, LANES), F32),
-            pltpu.VMEM((ext + 1, ring, LANES), F32),
+            pltpu.VMEM((ext + 2, 5, ring, LANES), F32),
+            pltpu.VMEM((ext + 2, 5, ring, LANES), F32),
+            pltpu.VMEM((2, ring, LANES), F32),
             pltpu.VMEM((2, ring, LANES), F32),
             pltpu.VMEM((ROWS, 2, ring, LANES), F32),
             pltpu.VMEM((ROWS, 2, ring, LANES), F32),

time: 36.5 us -> 36.7 us (level)
  no operation moved by 1% of the time
where the time goes in v5:
time: 36.7 us; the launch traced here: 36.5 us
  Pallas kernels  35.3 us (96%)
  between operations  0.64 us (2%)
  other arithmetic  0.63 us (2%)
    pallas_call x1, Pallas kernels, on_device(): pl.pallas_call(functools.partial(kernel, mesh.shape['gx'], mesh.shape['gy...  35.3 us

profile of v5, /device:TPU:1, one launch (start us, length us, event | category | flops | bytes accessed | tf_op | source)
XLA Modules:
  0.0 36.5 jit_solution(5735154827606921368)
XLA Ops:
  0.6 35.3 %shard_map.59 = f32[128,128]{1,0:T(8,128)S(1)} custom-call(f32[2304,128]{1,0:T(8,128)} %bitcast.2, f32[8,768]{1,0:T(8,128)} %bitcast.3, f32[768]{0:T(1024)} %weight_hbm.1, s32[768]{0:T(1024)} %group_hbm.1), custom_call_target="tpu_custom_call" | custom-call | tf_op jit(solution)/shard_map/pallas_call | solution.py:413
  35.9 0.6 %multiply_subtract_fusion = (f32[64,128]{1,0:T(8,128)}, f32[64,128]{1,0:T(8,128)}) fusion(f32[128,128]{1,0:T(8,128)S(1)} %shard_map.59), kind=kLoop, calls=%fused_computation | loop fusion | flops 16384 | bytes 131072 | tf_op jit(solution)/shard_map/sub | solution.py:461

commit v6 on v4

--- a/solution.py
+++ b/solution.py
@@ -177,9 +177,10 @@
                     piece = found[k * ring : (k + 1) * ring, half * LANES : (half + 1) * LANES]
                     target(ROWS * quad + k)[...] = piece
 
-    sent = fields * HALO
+    near = HALO - 1
+    sent = kpad * near
     for side in range(2):
-        recv_rows[side, pl.ds(sent, kpad * HALO - sent), :] = jnp.zeros((kpad * HALO - sent, LANES), F32)
+        recv_rows[side, pl.ds(sent, SUBLANES), :] = jnp.zeros((SUBLANES, LANES), F32)
     acc[...] = jnp.zeros_like(acc)
     pltpu.make_async_copy(field_hbm, fv.at[pl.ds(0, fields * rows)], load_sem.at[0]).wait()
 
@@ -190,9 +191,12 @@
     per_tile = LANES // HALO
     tiles = rows // per_tile
 
-    for r in range(HALO):
-        send_rows[0, pl.ds(r, kpad, stride=HALO), :] = fv[pl.ds(r, kpad, stride=apart), :]
-        send_rows[1, pl.ds(r, kpad, stride=HALO), :] = fv[pl.ds(rows - HALO + r, kpad, stride=apart), :]
+    for side in range(2):
+        for r in range(near):
+            row = r if side == 0 else rows - near + r
+            send_rows[side, pl.ds(r, kpad, stride=near), :] = fv[pl.ds(row, kpad, stride=apart), :]
+        row = near if side == 0 else rows - HALO
+        send_rows[side, pl.ds(fields * near, modes), :] = fv[pl.ds(row, modes, stride=apart), :]
     for t in range(tiles):
         low = [jnp.zeros((SUBLANES, LANES), F32)] * groups
         high = [jnp.zeros((SUBLANES, LANES), F32)] * groups
@@ -257,7 +261,12 @@
 
     for side, quad in ((1, 0), (0, quads - 1)):
         for k in range(ROWS):
-            x = recv_rows[side, pl.ds(k, kpad, stride=HALO), :]
+            outer = k == (near if side == 0 else 0)
+            if outer:
+                x = recv_rows[side, pl.ds(fields * near, 2 * SUBLANES), :]
+                x = jnp.concatenate([x, jnp.zeros((kpad - 2 * SUBLANES, LANES), F32)], axis=0)
+            else:
+                x = recv_rows[side, pl.ds(k - side, kpad, stride=near), :]
             lnat[quad % 2, pl.ds(k * ring, LANES), :] = turned(x)
         parameters(quad)
 
@@ -297,27 +306,27 @@
 
     tile = [pl.ds(SUBLANES * j, SUBLANES) for j in range(chunk)]
 
-    def advance(step, h, first):
-        cf = cfs[h].at[pl.ds(first, ROWS)]
-        u = us[h].at[pl.ds(first, ROWS + 1)]
-        cells = [kept.at[h]] + [u.at[k] for k in range(ROWS + 1)]
+    def advance(step, h, first, number):
+        cf = cfs[h].at[pl.ds(first, number)]
+        u = us[h].at[pl.ds(first, number + 1)]
+        cells = [kept.at[h]] + [u.at[k] for k in range(number + 1)]
 
         def column(j):
             return [ref[tile[j], :] for ref in cells]
 
         column_now = column(0)
         last = [ref[tile[chunk - 1], :] for ref in cells[1:-1]]
-        wrap = [column_now[k + 1] - pltpu.roll(last[k], 1, 0) for k in range(ROWS)]
+        wrap = [column_now[k + 1] - pltpu.roll(last[k], 1, 0) for k in range(number)]
         south = wrap
         for j in range(chunk):
             if j + 1 < chunk:
                 column_next = column(j + 1)
-                north = [column_next[k + 1] - column_now[k + 1] for k in range(ROWS)]
+                north = [column_next[k + 1] - column_now[k + 1] for k in range(number)]
             else:
                 column_next = None
                 north = [pltpu.roll(x, SUBLANES - 1, 0) for x in wrap]
-            east = [column_now[k + 1] - column_now[k] for k in range(ROWS + 1)]
-            for k in range(ROWS):
+            east = [column_now[k + 1] - column_now[k] for k in range(number + 1)]
+            for k in range(number):
                 c = [cf[k, m, tile[j], :] for m in range(4)]
                 new = column_now[k + 1] + (
                     (c[0] * east[k + 1] - c[1] * east[k]) + (c[2] * north[k] - c[3] * south[k])
@@ -333,7 +342,7 @@
                 else:
                     both[k, 0, tile[j], :] = one + part[k, 0, tile[j], :]
                     both[k, 1, tile[j], :] = two + part[k, 1, tile[j], :]
-            kept[h, tile[j], :] = column_now[ROWS]
+            kept[h, tile[j], :] = column_now[number]
             column_now, south = column_next, north
 
     def gather_sums(first):
@@ -344,19 +353,24 @@
                 old = jnp.where(mask, jnp.sum(both[k, m, tile[j], :], axis=1, keepdims=True), old)
             acc[tile[j], :] = old
 
-    for step, (start, turns) in {1: (0, quads), 2: (2, quads - 1), 3: (1, quads - 1), 4: (HALO, quads - 2)}.items():
+    for step in range(1, 5):
+        start, needed = step, ext - 2 * step
         for h in range(2):
             kept[h] = us[h][max(start - 1, 0)]
         if step == 4:
             both[...] = jnp.zeros_like(both)
 
-        @pl.loop(0, turns)
+        @pl.loop(0, needed // ROWS)
         def _(turn):
             first = start + ROWS * turn
             if step == 4:
                 gather_sums(first - HALO - ROWS)
             for h in range(2):
-                advance(step, h, first)
+                advance(step, h, first, ROWS)
+
+        if needed % ROWS:
+            for h in range(2):
+                advance(step, h, start + needed // ROWS * ROWS, needed % ROWS)
 
     gather_sums(rows - ROWS)
 
@@ -386,8 +400,8 @@
         out_specs=vmem,
         scratch_shapes=[
             pltpu.VMEM((kpad * (rows + SUBLANES), LANES), F32),
-            pltpu.VMEM((2, kpad * HALO, LANES), F32),
-            pltpu.VMEM((2, kpad * HALO, LANES), F32),
+            pltpu.VMEM((2, kpad * (HALO - 1) + SUBLANES, LANES), F32),
+            pltpu.VMEM((2, kpad * (HALO - 1) + SUBLANES, LANES), F32),
             pltpu.VMEM((2, tiles, kpad, LANES), F32),
             pltpu.VMEM((2, tiles, kpad, LANES), F32),
             pltpu.VMEM((4, SUBLANES, LANES), F32),

time: 36.5 us -> 36.5 us (level)
  no operation moved by 1% of the time
where the time goes in v6:
time: 36.5 us; the launch traced here: 36.3 us
  Pallas kernels  35 us (96%)
  between operations  0.64 us (2%)
  other arithmetic  0.63 us (2%)
    pallas_call x1, Pallas kernels, on_device(): pl.pallas_call(functools.partial(kernel, mesh.shape['gx'], mesh.shape['gy...  35 us

profile of v6, /device:TPU:1, one launch (start us, length us, event | category | flops | bytes accessed | tf_op | source)
XLA Modules:
  0.0 36.3 jit_solution(7690658978927209064)
XLA Ops:
  0.6 35.0 %shard_map.59 = f32[128,128]{1,0:T(8,128)S(1)} custom-call(f32[2304,128]{1,0:T(8,128)} %bitcast.2, f32[8,768]{1,0:T(8,128)} %bitcast.3, f32[768]{0:T(1024)} %weight_hbm.1, s32[768]{0:T(1024)} %group_hbm.1), custom_call_target="tpu_custom_call" | custom-call | tf_op jit(solution)/shard_map/pallas_call | solution.py:396
  35.7 0.6 %multiply_subtract_fusion = (f32[64,128]{1,0:T(8,128)}, f32[64,128]{1,0:T(8,128)}) fusion(f32[128,128]{1,0:T(8,128)S(1)} %shard_map.59), kind=kLoop, calls=%fused_computation | loop fusion | flops 16384 | bytes 131072 | tf_op jit(solution)/shard_map/sub | solution.py:445

commit v7 on v6

--- a/solution.py
+++ b/solution.py
@@ -13,7 +13,8 @@
 SUBLANES = 8
 SLOTS = 256
 ROWS = 4
-EARLY = 4
+EARLY = 14
+RING = 4
 MESH = pl.DeviceIdType.MESH
 F32 = jnp.float32
 BF16 = jnp.bfloat16
@@ -222,7 +223,10 @@
 
     turn_rows(1)
 
-    @pl.loop(1, 1 + EARLY)
+    x_chip, y_chip = lax.rem(gy, RING), 2 * (gy // RING) + gx // RING
+    early = jnp.clip(EARLY - x_chip - y_chip - 2 * lax.rem(gx, RING), 0, quads - 3)
+
+    @pl.loop(1, 1 + early)
     def _(quad):
         parameters(quad)
         turn_rows(quad + 1)
@@ -249,7 +253,7 @@
         remote(3, send_cols.at[1], recv_cols.at[1], (core, gx, yn)),
     ]
 
-    @pl.loop(1 + EARLY, quads - 2)
+    @pl.loop(1 + early, quads - 2)
     def _(quad):
         parameters(quad)
         turn_rows(quad + 1)

time: 36.5 us -> 36 us (0.986)
  Pallas kernels: 35 us -> 34.6 us
    pallas_call x1, Pallas kernels: 35 us -> 34.6 us  [on_device(): pl.pallas_call(functools.partial(kernel, mesh.shape['gx'], mesh.shape['gy...]
where the time goes in v7:
time: 36 us; the launch traced here: 35.9 us
  Pallas kernels  34.6 us (96%)
  between operations  0.64 us (2%)
  other arithmetic  0.63 us (2%)
    pallas_call x1, Pallas kernels, on_device(): pl.pallas_call(functools.partial(kernel, mesh.shape['gx'], mesh.shape['gy...  34.6 us

profile of v7, /device:TPU:1, one launch (start us, length us, event | category | flops | bytes accessed | tf_op | source)
XLA Modules:
  0.0 35.9 jit_solution(13237822225234747125)
XLA Ops:
  0.6 34.6 %shard_map.59 = f32[128,128]{1,0:T(8,128)S(1)} custom-call(f32[2304,128]{1,0:T(8,128)} %bitcast.2, f32[8,768]{1,0:T(8,128)} %bitcast.3, f32[768]{0:T(1024)} %weight_hbm.1, s32[768]{0:T(1024)} %group_hbm.1), custom_call_target="tpu_custom_call" | custom-call | tf_op jit(solution)/shard_map/pallas_call | solution.py:400
  35.2 0.6 %multiply_subtract_fusion = (f32[64,128]{1,0:T(8,128)}, f32[64,128]{1,0:T(8,128)}) fusion(f32[128,128]{1,0:T(8,128)S(1)} %shard_map.59), kind=kLoop, calls=%fused_computation | loop fusion | flops 16384 | bytes 131072 | tf_op jit(solution)/shard_map/sub | solution.py:449

commit v8 on v7

--- a/solution.py
+++ b/solution.py
@@ -13,7 +13,7 @@
 SUBLANES = 8
 SLOTS = 256
 ROWS = 4
-EARLY = 14
+EARLY = 12
 RING = 4
 MESH = pl.DeviceIdType.MESH
 F32 = jnp.float32

time: 36 us -> 35 us (0.972)
  Pallas kernels: 34.6 us -> 33.6 us
    pallas_call x1, Pallas kernels: 34.6 us -> 33.6 us  [on_device(): pl.pallas_call(functools.partial(kernel, mesh.shape['gx'], mesh.shape['gy...]
where the time goes in v8:
time: 35 us; the launch traced here: 34.8 us
  Pallas kernels  33.6 us (96%)
  between operations  0.64 us (2%)
  other arithmetic  0.63 us (2%)
    pallas_call x1, Pallas kernels, on_device(): pl.pallas_call(functools.partial(kernel, mesh.shape['gx'], mesh.shape['gy...  33.6 us

profile of v8, /device:TPU:1, one launch (start us, length us, event | category | flops | bytes accessed | tf_op | source)
XLA Modules:
  0.0 34.8 jit_solution(4754386685925352237)
XLA Ops:
  0.6 33.6 %shard_map.59 = f32[128,128]{1,0:T(8,128)S(1)} custom-call(f32[2304,128]{1,0:T(8,128)} %bitcast.2, f32[8,768]{1,0:T(8,128)} %bitcast.3, f32[768]{0:T(1024)} %weight_hbm.1, s32[768]{0:T(1024)} %group_hbm.1), custom_call_target="tpu_custom_call" | custom-call | tf_op jit(solution)/shard_map/pallas_call | solution.py:400
  34.2 0.6 %multiply_subtract_fusion = (f32[64,128]{1,0:T(8,128)}, f32[64,128]{1,0:T(8,128)}) fusion(f32[128,128]{1,0:T(8,128)S(1)} %shard_map.59), kind=kLoop, calls=%fused_computation | loop fusion | flops 16384 | bytes 131072 | tf_op jit(solution)/shard_map/sub | solution.py:449
